TPU v7x, 32 devices: a whole 2x2x4 slice. The times are simulated.
32 devices in a mesh: lon: 8 (over y, x, core), lat: 4 (over z).
Axes of the slice: x: 2, y: 2, z: 4, core: 2. Of those that a mesh axis runs over, the one named last changes fastest.
Arguments:
- normed: bfloat16 [8, 96, 192, 192], P(None, 'lat', 'lon'), may hold values from -6 to 6
- cotangent: bfloat16 [8, 96, 192, 192], P(None, 'lat', 'lon'), may hold values from -6 to 6
- weight_qkv: bfloat16 [192, 576], replicated, may hold values from -0.4375 to 0.4375
- weight_proj: bfloat16 [192, 192], replicated, may hold values from -0.4375 to 0.4375
- bias_table: bfloat16 [64, 6, 20736], P('lat'), may hold values from -6 to 390
Outputs:
- input_grad: bfloat16 [8, 96, 192, 192], P(None, 'lat', 'lon')
- qkv_grad: float32 [192, 576], replicated
- proj_grad: float32 [192, 192], replicated
- bias_grad: float32 [64, 6, 20736], P('lat')
All inputs are finite; a program needn't handle non-finite values.
Results may differ from a plain program's by a relative error of at most 0.019.
Values may be sent and summed in bfloat16 or wider, within the bound.
A program may use at most 192 MiB of HBM per device.

v0:
```python
import jax
import jax.numpy as jnp
from jax import lax
from jax.sharding import PartitionSpec as P

HEADS = 6
WIN_Z = 2
WIN_LAT = 6
WIN_LON = 12
WTOK = 144


def from_behind(block, axis, distance):
    devices = range(lax.axis_size(axis))
    route = [((i - distance) % len(devices), i) for i in devices]
    return lax.ppermute(block, axis, route)


def passed_along(block, axis, distance):
    devices = range(lax.axis_size(axis))
    route = [(i - distance, i) for i in devices if i - distance in devices]
    return lax.ppermute(block, axis, route)


def window_split(grid_field):
    levels, height, breadth = grid_field.shape[:3]
    trailing_dims = grid_field.shape[3:]
    shaped = grid_field.reshape(
        (levels // WIN_Z, WIN_Z, height // WIN_LAT, WIN_LAT, breadth // WIN_LON, WIN_LON)
        + trailing_dims
    )
    axes_order = (0, 2, 4, 1, 3, 5) + tuple(range(6, 6 + len(trailing_dims)))
    return shaped.transpose(axes_order).reshape((-1, WTOK) + trailing_dims)


def window_merge(windowed, levels, height, breadth):
    channels = windowed.shape[-1]
    shaped = windowed.reshape(
        levels // WIN_Z, height // WIN_LAT, breadth // WIN_LON, WIN_Z, WIN_LAT, WIN_LON, channels
    )
    return shaped.transpose(0, 3, 1, 4, 2, 5, 6).reshape(levels, height, breadth, channels)


def window_backward(
    block_in, block_cot, block_region, block_live, block_types, bias_rows, weight_qkv, weight_proj
):
    windows = block_in.shape[0]
    channels = block_in.shape[2]
    head_dim = channels // HEADS
    softmax_scale = head_dim ** (-0.5)
    high = lax.Precision.HIGHEST
    f32 = jnp.float32
    projected = jnp.einsum("bnc,cf->bnf", block_in, weight_qkv, preferred_element_type=f32).astype(
        jnp.bfloat16
    )
    projected = projected.reshape(windows, WTOK, 3, HEADS, head_dim)
    queries = projected[:, :, 0]
    key_rows = projected[:, :, 1]
    values = projected[:, :, 2]
    bias_add = jnp.dot(
        block_types.astype(jnp.bfloat16), bias_rows, preferred_element_type=f32
    ).reshape(windows, HEADS, WTOK, WTOK)
    scores = (
        jnp.einsum("bqhd,bkhd->bhqk", queries, key_rows, preferred_element_type=f32) * softmax_scale
        + bias_add
    )
    allowed = (block_region[:, :, None] == block_region[:, None, :]) & (
        block_live[:, :, None] == block_live[:, None, :]
    )
    allowed = allowed[:, None]
    peak_score = jnp.max(jnp.where(allowed, scores, -1e30), axis=-1, keepdims=True)
    exp_terms = jnp.where(allowed, jnp.exp(scores - peak_score), 0.0)
    attn_probs = exp_terms / jnp.sum(exp_terms, axis=-1, keepdims=True)
    probs_b = attn_probs.astype(jnp.bfloat16)
    mixed = jnp.einsum("bhqk,bkhd->bqhd", probs_b, values, preferred_element_type=f32).astype(
        jnp.bfloat16
    )
    mixed = mixed.reshape(windows, WTOK, channels)
    grad_proj = jnp.einsum("bnc,bnf->cf", mixed, block_cot, preferred_element_type=f32)
    mixed_grad = jnp.einsum(
        "bnf,cf->bnc", block_cot, weight_proj, preferred_element_type=f32
    ).astype(jnp.bfloat16)
    mixed_grad = mixed_grad.reshape(windows, WTOK, HEADS, head_dim)
    prob_grad = jnp.einsum("bqhd,bkhd->bhqk", mixed_grad, values, preferred_element_type=f32)
    row_delta = jnp.sum(attn_probs * prob_grad, axis=-1, keepdims=True)
    score_grad = attn_probs * (prob_grad - row_delta)
    grad_bias = jnp.dot(
        block_types.T, score_grad.reshape(windows, -1), precision=high, preferred_element_type=f32
    )
    score_grad_b = score_grad.astype(jnp.bfloat16)
    query_grad = (
        jnp.einsum("bhqk,bkhd->bqhd", score_grad_b, key_rows, preferred_element_type=f32)
        * softmax_scale
    ).astype(jnp.bfloat16)
    key_grad = (
        jnp.einsum("bhqk,bqhd->bkhd", score_grad_b, queries, preferred_element_type=f32)
        * softmax_scale
    ).astype(jnp.bfloat16)
    value_grad = jnp.einsum(
        "bhqk,bqhd->bkhd", probs_b, mixed_grad, preferred_element_type=f32
    ).astype(jnp.bfloat16)
    cols_grad = jnp.stack([query_grad, key_grad, value_grad], axis=2).reshape(
        windows, WTOK, 3 * channels
    )
    grad_qkv = jnp.einsum("bnc,bnf->cf", block_in, cols_grad, preferred_element_type=f32)
    grad_in = jnp.einsum("bnf,cf->bnc", cols_grad, weight_qkv, preferred_element_type=f32).astype(
        jnp.bfloat16
    )
    return (grad_in, grad_qkv, grad_proj, grad_bias)


def local(normed, cotangent, weight_qkv, weight_proj, bias_table):
    levels, height, breadth, channels = normed.shape
    level_shift = WIN_Z // 2
    lat_shift = WIN_LAT // 2
    lon_shift = WIN_LON // 2
    normed = jnp.roll(normed, -level_shift, axis=0)
    cotangent = jnp.roll(cotangent, -level_shift, axis=0)
    across = from_behind((normed[:, :, :lon_shift], cotangent[:, :, :lon_shift]), "lon", -1)
    wide_in = jnp.concatenate([normed[:, :, lon_shift:], across[0]], axis=2)
    wide_cot = jnp.concatenate([cotangent[:, :, lon_shift:], across[1]], axis=2)
    upward = passed_along((wide_in[:, :lat_shift], wide_cot[:, :lat_shift]), "lat", -1)
    frame_in = jnp.concatenate([wide_in[:, lat_shift:], upward[0]], axis=1)
    frame_cot = jnp.concatenate([wide_cot[:, lat_shift:], upward[1]], axis=1)
    is_last = lax.axis_index("lat") == lax.axis_size("lat") - 1
    row_index = jnp.arange(height, dtype=jnp.int32)
    live_rows = jnp.logical_not(is_last & (row_index >= height - lat_shift))
    live_field = jnp.broadcast_to(live_rows[None, :, None], (levels, height, breadth))
    level_index = jnp.arange(levels, dtype=jnp.int32)
    wrapped_levels = (level_index >= levels - level_shift).astype(jnp.int32)
    wrapped_field = jnp.broadcast_to(wrapped_levels[:, None, None], (levels, height, breadth))
    level_windows = levels // WIN_Z
    lat_windows = height // WIN_LAT
    lon_windows = breadth // WIN_LON
    types_local = level_windows * lat_windows
    level_part = jnp.arange(level_windows, dtype=jnp.int32)[:, None, None]
    lat_part = jnp.arange(lat_windows, dtype=jnp.int32)[None, :, None]
    kinds = jnp.broadcast_to(
        lat_part * level_windows + level_part, (level_windows, lat_windows, lon_windows)
    )
    onehot = (
        kinds.reshape(-1)[:, None] == jnp.arange(types_local, dtype=jnp.int32)[None, :]
    ).astype(jnp.float32)
    bias_rows = bias_table.reshape(types_local, -1)
    framed_in = window_split(frame_in)
    window_total = framed_in.shape[0]
    block_size = max((divisor for divisor in range(1, 17) if window_total % divisor == 0))
    blocks = window_total // block_size

    def regroup(array):
        return array.reshape((blocks, block_size) + array.shape[1:])

    def step_block(totals, pieces):
        grad_in, grad_qkv, grad_proj, grad_bias = window_backward(
            pieces[0],
            pieces[1],
            pieces[2],
            pieces[3],
            pieces[4],
            bias_rows,
            weight_qkv,
            weight_proj,
        )
        return ((totals[0] + grad_qkv, totals[1] + grad_proj, totals[2] + grad_bias), grad_in)

    start = (
        jnp.zeros((channels, 3 * channels), jnp.float32),
        jnp.zeros((channels, channels), jnp.float32),
        jnp.zeros((types_local, HEADS * WTOK * WTOK), jnp.float32),
    )
    pieces = (
        regroup(framed_in),
        regroup(window_split(frame_cot)),
        regroup(window_split(wrapped_field)),
        regroup(window_split(live_field)),
        regroup(onehot),
    )
    totals, grads = lax.scan(step_block, start, pieces)
    framed_grad = window_merge(grads.reshape(window_total, WTOK, channels), levels, height, breadth)
    returned = passed_along(framed_grad[:, height - lat_shift :], "lat", 1)
    wide_grad = jnp.concatenate([returned, framed_grad[:, : height - lat_shift]], axis=1)
    sideways = from_behind(wide_grad[:, :, breadth - lon_shift :], "lon", 1)
    shifted_grad = jnp.concatenate([sideways, wide_grad[:, :, : breadth - lon_shift]], axis=2)
    input_grad = jnp.roll(shifted_grad, level_shift, axis=0)
    lat_qkv, lat_proj = (
        lax.psum(totals[0].astype(jnp.bfloat16), "lat").astype(jnp.float32),
        lax.psum(totals[1].astype(jnp.bfloat16), "lat").astype(jnp.float32),
    )
    bias_grad, qkv_grad, proj_grad = (
        lax.psum(totals[2].astype(jnp.bfloat16), "lon").astype(jnp.float32),
        lax.psum(lat_qkv.astype(jnp.bfloat16), "lon").astype(jnp.float32),
        lax.psum(lat_proj.astype(jnp.bfloat16), "lon").astype(jnp.float32),
    )
    return (input_grad, qkv_grad, proj_grad, bias_grad.reshape(types_local, HEADS, WTOK * WTOK))


def solution(mesh):
    in_specs = (
        P(None, "lat", "lon", None),
        P(None, "lat", "lon", None),
        P(),
        P(),
        P("lat", None, None),
    )
    out_specs = (P(None, "lat", "lon", None), P(), P(), P("lat", None, None))
    return jax.shard_map(local, mesh=mesh, in_specs=in_specs, out_specs=out_specs, check_vma=False)
```

profile of v0, /device:TPU:0, one launch (start us, length us, event | category | flops | bytes accessed | tf_op | source)
XLA Modules:
  0.0 629.4 jit_solution(3365991301374217343)
XLA Ops:
  68.9 396.9 %while.17 = (s32[]{:T(128)}, f32[192,576]{1,0:T(8,128)}, f32[192,192]{1,0:T(8,128)}, f32[16,124416]{1,0:T(8,128)}, bf16[2,16,144,192]{3,1,0,2:T(8,128)(2,1)}, /*...) while((s32[]{:T(128)}, f32[192,576]{1,0:T(8,128)}, ...), condition=%wide.region_4.5_spmd.clone, body=%wide.region_0.4_spmd.clone.sunk | while | flops 3127491072 | bytes 382142976 | solution.py:178
  72.4 15.1 %dot_general.59 = bf16[6,144,144,16]{2,1,0,3:T(8,128)(2,1)} reshape(bf16[124416,16]{0,1:T(8,128)(2,1)} %bitcast.192) | data formatting | bytes 7962624 | tf_op jit(solution)/shard_map/while/body/eval_jaxpr/dot_general | solution.py:60
  87.5 12.4 %fusion.128 = f32[16,6,144,144]{3,0,2,1:T(8,128)} fusion(bf16[6,144,144,16]{2,1,0,3:T(8,128)(2,1)} %dot_general.59, f32[2,16,16]{2,1,0:T(8,128)S(1)} %get-tuple-element.332, s32[]{:T(128)S(6)} %copy.169), kind=kOutput, calls=%fused_computation.8.clone.1 | convolution fusion | flops 63700992 | bytes 11948036 | tf_op jit(solution)/shard_map/while/body/eval_jaxpr/dot_general | solution.py:60
  99.8 17.0 %copy.157 = f32[16,6,144,144]{2,3,1,0:T(8,128)} copy(f32[16,6,144,144]{3,0,2,1:T(8,128)} %fusion.128) | data formatting | bytes 15925248 | tf_op jit(solution)/shard_map/while/body/eval_jaxpr/dot_general | solution.py:60
  124.3 13.1 %multiply_add_fusion.2 = f32[16,6,144,144]{2,3,1,0:T(8,128)} fusion(f32[16,6,144,144]{2,3,1,0:T(8,128)} %copy.157, bf16[16,144,3,6,32]{1,4,3,2,0:T(8,128)(2,1)} %bitcast.182), kind=kOutput, calls=%fused_computation.7.clone.1 | convolution fusion | flops 131383296 | bytes 25264128 | tf_op jit(solution)/shard_map/while/body/eval_jaxpr/bqhd,bkhd->bhqk/dot_general | solution.py:64
  138.5 15.3 %fusion.129 = (f32[16,6,144]{2,1,0:T(8,128)S(1)}, f32[16,6,144,144]{2,3,1,0:T(8,128)}) fusion(f32[16,6,144,144]{2,3,1,0:T(8,128)} %multiply_add_fusion.2, pred[16,144,144]{1,2,0:T(8,128)(4,1)S(1)} %compare_and_fusion.2), kind=kOutput, calls=%fused_computation.93.clone.1 | output fusion | flops 7962767 | bytes 16312320 | tf_op jit(solution)/shard_map/while/body/eval_jaxpr/sub | solution.py:72
  153.8 8.0 %fusion.130 = bf16[16,144,1,6,32]{1,4,3,0,2:T(8,128)(2,1)S(1)} fusion(bf16[16,144,6,32]{1,3,2,0:T(8,128)(2,1)} %bitcast.193, f32[16,6,144,144]{2,3,1,0:T(8,128)} %get-tuple-element.289, f32[16,6,144]{2,1,0:T(8,128)S(1)} %get-tuple-element.290), kind=kOutput, calls=%fused_computation.33.clone.1 | convolution fusion | flops 131825664 | bytes 9787392 | tf_op jit(solution)/shard_map/while/body/eval_jaxpr/bhqk,bqhd->bkhd/dot_general | solution.py:99
  163.4 9.7 %multiply_reduce_fusion.2 = (f32[16,6,144]{2,1,0:T(8,128)S(1)}, f32[16,6,144,144]{2,3,1,0:T(8,128)}) fusion(f32[16,6,144,144]{2,3,1,0:T(8,128)S(1)} %copy-done.1, f32[16,6,144]{2,1,0:T(8,128)S(1)} %get-tuple-element.290, bf16[16,144,6,32]{1,3,2,0:T(8,128)(2,1)} %bitcast.194, bf16[16,144,3,6,32]{1,4,3,2,0:T(8,128)(2,1)} %bitcast.183), kind=kOutput, calls=%fused_computation.3.clone.1 | convolution fusion | flops 133360128 | bytes 19181568 | tf_op jit(solution)/shard_map/while/body/eval_jaxpr/bqhd,bkhd->bhqk/dot_general | solution.py:84
  173.1 10.1 %subtract_multiply_fusion.2 = f32[16,6,144,144]{2,3,1,0:T(8,128)S(1)} fusion(f32[16,6,144,144]{2,3,1,0:T(8,128)} %get-tuple-element.291, f32[16,6,144]{2,1,0:T(8,128)S(1)} %get-tuple-element.292, f32[16,6,144,144]{2,3,1,0:T(8,128)} %get-tuple-element.289, f32[16,6,144]{2,1,0:T(8,128)S(1)} %get-tuple-element.290), kind=kLoop, calls=%fused_computation.2.clone.1 | loop fusion | flops 5971968 | bytes 23998464 | tf_op jit(solution)/shard_map/while/body/eval_jaxpr/mul | solution.py:86
  199.7 6.8 %fusion.134 = bf16[16,6,32,144]{3,2,1,0:T(8,128)(2,1)S(1)} fusion(bf16[16,144,3,6,32]{1,4,3,2,0:T(8,128)(2,1)} %bitcast.186, f32[16,6,144,144]{2,3,1,0:T(8,128)} %get-tuple-element.289, f32[16,6,144]{2,1,0:T(8,128)S(1)} %copy-done.8), kind=kOutput, calls=%fused_computation.27.clone.1 | convolution fusion | flops 131825664 | bytes 16668672 | tf_op jit(solution)/shard_map/while/body/eval_jaxpr/bhqk,bkhd->bqhd/dot_general | solution.py:75
  207.2 17.1 %copy.160 = f32[16,6,144,144]{3,2,1,0:T(8,128)} copy(f32[16,6,144,144]{2,3,1,0:T(8,128)} %copy-done) | data formatting | bytes 15925248 | tf_op jit(solution)/shard_map/while/body/eval_jaxpr/mul | solution.py:86
  224.3 23.2 %reshape.132 = f32[16,124416]{1,0:T(8,128)} reshape(f32[16,6,144,144]{3,2,1,0:T(8,128)} %copy.160) | data formatting | bytes 15925248 | tf_op jit(solution)/shard_map/while/body/eval_jaxpr/reshape | solution.py:88
  247.5 11.2 %convolution_add_fusion.2 = f32[16,124416]{1,0:T(8,128)} fusion(f32[16,124416]{1,0:T(8,128)} %reshape.132, f32[16,124416]{1,0:T(8,128)} %get-tuple-element.311, pred[]{:T(512)S(6)} %compare.3, f32[2,16,16]{2,1,0:T(8,128)S(1)} %get-tuple-element.332, s32[]{:T(128)S(6)} %copy.169), kind=kOutput, calls=%fused_computation.1.clone.1 | convolution fusion | flops 386187264 | bytes 23896068 | tf_op jit(solution)/shard_map/while/body/eval_jaxpr/dot_general | solution.py:87
  265.9 15.1 %dot_general.59 = bf16[6,144,144,16]{2,1,0,3:T(8,128)(2,1)} reshape(bf16[124416,16]{0,1:T(8,128)(2,1)} %bitcast.192) | data formatting | bytes 7962624 | tf_op jit(solution)/shard_map/while/body/eval_jaxpr/dot_general | solution.py:60
  281.0 12.4 %fusion.128 = f32[16,6,144,144]{3,0,2,1:T(8,128)} fusion(bf16[6,144,144,16]{2,1,0,3:T(8,128)(2,1)} %dot_general.59, f32[2,16,16]{2,1,0:T(8,128)S(1)} %get-tuple-element.332, s32[]{:T(128)S(6)} %copy.169), kind=kOutput, calls=%fused_computation.8.clone.1 | convolution fusion | flops 63700992 | bytes 11948036 | tf_op jit(solution)/shard_map/while/body/eval_jaxpr/dot_general | solution.py:60
  293.4 17.0 %copy.157 = f32[16,6,144,144]{2,3,1,0:T(8,128)} copy(f32[16,6,144,144]{3,0,2,1:T(8,128)} %fusion.128) | data formatting | bytes 15925248 | tf_op jit(solution)/shard_map/while/body/eval_jaxpr/dot_general | solution.py:60
  317.6 13.1 %multiply_add_fusion.2 = f32[16,6,144,144]{2,3,1,0:T(8,128)} fusion(f32[16,6,144,144]{2,3,1,0:T(8,128)} %copy.157, bf16[16,144,3,6,32]{1,4,3,2,0:T(8,128)(2,1)} %bitcast.182), kind=kOutput, calls=%fused_computation.7.clone.1 | convolution fusion | flops 131383296 | bytes 25264128 | tf_op jit(solution)/shard_map/while/body/eval_jaxpr/bqhd,bkhd->bhqk/dot_general | solution.py:64
  331.7 15.3 %fusion.129 = (f32[16,6,144]{2,1,0:T(8,128)S(1)}, f32[16,6,144,144]{2,3,1,0:T(8,128)}) fusion(f32[16,6,144,144]{2,3,1,0:T(8,128)} %multiply_add_fusion.2, pred[16,144,144]{1,2,0:T(8,128)(4,1)S(1)} %compare_and_fusion.2), kind=kOutput, calls=%fused_computation.93.clone.1 | output fusion | flops 7962767 | bytes 16312320 | tf_op jit(solution)/shard_map/while/body/eval_jaxpr/sub | solution.py:72
  347.1 8.0 %fusion.130 = bf16[16,144,1,6,32]{1,4,3,0,2:T(8,128)(2,1)S(1)} fusion(bf16[16,144,6,32]{1,3,2,0:T(8,128)(2,1)} %bitcast.193, f32[16,6,144,144]{2,3,1,0:T(8,128)} %get-tuple-element.289, f32[16,6,144]{2,1,0:T(8,128)S(1)} %get-tuple-element.290), kind=kOutput, calls=%fused_computation.33.clone.1 | convolution fusion | flops 131825664 | bytes 9787392 | tf_op jit(solution)/shard_map/while/body/eval_jaxpr/bhqk,bqhd->bkhd/dot_general | solution.py:99
  356.6 9.7 %multiply_reduce_fusion.2 = (f32[16,6,144]{2,1,0:T(8,128)S(1)}, f32[16,6,144,144]{2,3,1,0:T(8,128)}) fusion(f32[16,6,144,144]{2,3,1,0:T(8,128)S(1)} %copy-done.1, f32[16,6,144]{2,1,0:T(8,128)S(1)} %get-tuple-element.290, bf16[16,144,6,32]{1,3,2,0:T(8,128)(2,1)} %bitcast.194, bf16[16,144,3,6,32]{1,4,3,2,0:T(8,128)(2,1)} %bitcast.183), kind=kOutput, calls=%fused_computation.3.clone.1 | convolution fusion | flops 133360128 | bytes 19181568 | tf_op jit(solution)/shard_map/while/body/eval_jaxpr/bqhd,bkhd->bhqk/dot_general | solution.py:84
  366.3 10.1 %subtract_multiply_fusion.2 = f32[16,6,144,144]{2,3,1,0:T(8,128)S(1)} fusion(f32[16,6,144,144]{2,3,1,0:T(8,128)} %get-tuple-element.291, f32[16,6,144]{2,1,0:T(8,128)S(1)} %get-tuple-element.292, f32[16,6,144,144]{2,3,1,0:T(8,128)} %get-tuple-element.289, f32[16,6,144]{2,1,0:T(8,128)S(1)} %get-tuple-element.290), kind=kLoop, calls=%fused_computation.2.clone.1 | loop fusion | flops 5971968 | bytes 23998464 | tf_op jit(solution)/shard_map/while/body/eval_jaxpr/mul | solution.py:86
  393.1 6.8 %fusion.134 = bf16[16,6,32,144]{3,2,1,0:T(8,128)(2,1)S(1)} fusion(bf16[16,144,3,6,32]{1,4,3,2,0:T(8,128)(2,1)} %bitcast.186, f32[16,6,144,144]{2,3,1,0:T(8,128)} %get-tuple-element.289, f32[16,6,144]{2,1,0:T(8,128)S(1)} %copy-done.8), kind=kOutput, calls=%fused_computation.27.clone.1 | convolution fusion | flops 131825664 | bytes 16668672 | tf_op jit(solution)/shard_map/while/body/eval_jaxpr/bhqk,bkhd->bqhd/dot_general | solution.py:75
  400.5 17.1 %copy.160 = f32[16,6,144,144]{3,2,1,0:T(8,128)} copy(f32[16,6,144,144]{2,3,1,0:T(8,128)} %copy-done) | data formatting | bytes 15925248 | tf_op jit(solution)/shard_map/while/body/eval_jaxpr/mul | solution.py:86
  417.6 23.2 %reshape.132 = f32[16,124416]{1,0:T(8,128)} reshape(f32[16,6,144,144]{3,2,1,0:T(8,128)} %copy.160) | data formatting | bytes 15925248 | tf_op jit(solution)/shard_map/while/body/eval_jaxpr/reshape | solution.py:88
  440.8 13.3 %convolution_add_fusion.2 = f32[16,124416]{1,0:T(8,128)} fusion(f32[16,124416]{1,0:T(8,128)} %reshape.132, f32[16,124416]{1,0:T(8,128)} %get-tuple-element.311, pred[]{:T(512)S(6)} %compare.3, f32[2,16,16]{2,1,0:T(8,128)S(1)} %get-tuple-element.332, s32[]{:T(128)S(6)} %copy.169), kind=kOutput, calls=%fused_computation.1.clone.1 | convolution fusion | flops 386187264 | bytes 23896068 | tf_op jit(solution)/shard_map/while/body/eval_jaxpr/dot_general | solution.py:87
  469.2 5.5 convert_element_type.82
  474.8 9.0 %reshape.117 = bf16[16,6,20736]{2,1,0:T(8,128)(2,1)} reshape(bf16[16,124416]{1,0:T(8,128)(2,1)} %convert_element_type.82) | data formatting | bytes 7962624 | tf_op jit(solution)/shard_map/reshape | solution.py:194
  483.8 21.9 %all-reduce.7.cloned.1.call-done = (bf16[192,576]{1,0:T(8,128)(2,1)}, bf16[192,192]{1,0:T(8,128)(2,1)}) async-done(((bf16[192,576]{1,0:T(8,128)(2,1)}, bf16[192,192]{1,0:T(8,128)(2,1)}), (bf16[192,576]{1,0:T(8,128)(2,1)}, bf16[192,192]{1,0:T(8,128)(2,1)})) %all-reduce.7.cloned.1.call-update) | async-done | bytes 294928 | tf_op jit(solution)/shard_map/psum | solution.py:186
  514.5 5.2 reshape.116
  528.2 19.4 %collective-permute-done.5 = bf16[8,24,6,192]{3,0,2,1:T(8,128)(2,1)S(1)} collective-permute-done((bf16[8,24,6,192]{3,0,2,1:T(8,128)(2,1)S(1)}, bf16[8,24,6,192]{3,0,2,1:T(8,128)(2,1)S(1)}, u32[]{:S(2)}, u32[]{:S(2)}) %collective-permute-start.5) | collective-permute-done | bytes 442400 | tf_op jit(solution)/shard_map/ppermute | solution.py:16
  550.8 61.7 %all-reduce.5.cloned.1.call-done = (bf16[16,6,20736]{2,1,0:T(8,128)(2,1)}, bf16[192,576]{1,0:T(8,128)(2,1)}, bf16[192,192]{1,0:T(8,128)(2,1)}) async-done(((bf16[16,6,20736]{2,1,0:T(8,128)(2,1)}, bf16[192,576]{1,0:T(8,128)(2,1)}, bf16[192,192]{1,0:T(8,128)(2,1)}), (bf16[16,6,20736]{2,1,0:T(8,128)(2,1)}, bf16[192,576]{1,0:T(8,128)(2,1)}, bf16[192,192]{1,0:T(8,128)(2,1)})) %all-reduce.5.cloned.1.call-update) | async-done | bytes 4276240 | tf_op jit(solution)/shard_map/psum | solution.py:190
  615.8 6.5 %copy.117 = f32[16,6,20736]{2,0,1:T(8,128)} copy(bf16[16,6,20736]{2,1,0:T(8,128)(2,1)} %get-tuple-element.197) | data formatting | bytes 11943936
  (192 shorter events, 156.0 us)
Async XLA Ops:
  7.2 498.5 %all-reduce.7.cloned.1.call-start = ((), (), s32[]{:S(2)}) async-start(), calls=%async_computation.1 | async-start | bytes 688128 | tf_op jit(solution)/shard_map/psum | solution.py:186
  10.1 20.1 %collective-permute-start = (bf16[8,24,6,192]{3,1,2,0:T(8,128)(2,1)}, bf16[8,24,6,192]{3,1,2,0:T(8,128)(2,1)}, u32[]{:S(2)}, u32[]{:S(2)}) collective-permute-start(bf16[8,24,6,192]{3,1,2,0:T(8,128)(2,1)} %slice.92), channel_id=1, source_target_pairs={{4,0},{8,4},{12,8},{16,12},{20,16},{24,20},{28,24},{0,28},{5,1},{9... | collective-permute-start | bytes 1327112 | tf_op jit(solution)/shard_map/ppermute | solution.py:16
  16.8 15.9 %collective-permute-start.2 = (bf16[8,24,6,192]{3,1,2,0:T(8,128)(2,1)}, bf16[8,24,6,192]{3,1,2,0:T(8,128)(2,1)}, u32[]{:S(2)}, u32[]{:S(2)}) collective-permute-start(bf16[8,24,6,192]{3,1,2,0:T(8,128)(2,1)} %slice.96), channel_id=1, source_target_pairs={{4,0},{8,4},{12,8},{16,12},{20,16},{24,20},{28,24},{0,28},{5,1},{9... | collective-permute-start | bytes 1327112 | tf_op jit(solution)/shard_map/ppermute | solution.py:16
  31.4 11.8 %collective-permute-start.1 = (bf16[8,3,24,192]{3,2,1,0:T(8,128)(2,1)S(1)}, bf16[8,3,24,192]{3,2,1,0:T(8,128)(2,1)S(1)}, u32[]{:S(2)}, u32[]{:S(2)}) collective-permute-start(bf16[8,3,24,192]{3,2,1,0:T(8,128)(2,1)S(1)} %copy.101), channel_id=1, source_target_pairs={{1,0},{2,1},{3,2},{5,4},{6,5},{7,6},{9,8},{10,9},{11,10},{13,12},{... | collective-permute-start | bytes 663560 | tf_op jit(solution)/shard_map/ppermute | solution.py:22
  34.5 18.7 %collective-permute-start.3 = (bf16[8,3,24,192]{3,2,1,0:T(8,128)(2,1)}, bf16[8,3,24,192]{3,2,1,0:T(8,128)(2,1)}, u32[]{:S(2)}, u32[]{:S(2)}) collective-permute-start(bf16[8,3,24,192]{3,2,1,0:T(8,128)(2,1)} %copy.108), channel_id=1, source_target_pairs={{1,0},{2,1},{3,2},{5,4},{6,5},{7,6},{9,8},{10,9},{11,10},{13,12},{... | collective-permute-start | bytes 663560 | tf_op jit(solution)/shard_map/ppermute | solution.py:22
  69.2 18.3 %copy-start.3 = (bf16[2,16,144,192]{3,2,1,0:T(8,128)(2,1)}, bf16[2,16,144,192]{3,2,1,0:T(8,128)(2,1)S(1)}, u32[]{:S(2)}) copy-start(bf16[2,16,144,192]{3,2,1,0:T(8,128)(2,1)S(1)} %get-tuple-element.334) | copy-start | bytes 5308420 | tf_op jit(solution)/shard_map/while
  99.8 17.0 %copy-start.5 = (bf16[192,576]{1,0:T(8,128)(2,1)S(1)}, bf16[192,576]{1,0:T(8,128)(2,1)}, u32[]{:S(2)}) copy-start(bf16[192,576]{1,0:T(8,128)(2,1)} %get-tuple-element.329) | copy-start | bytes 663556 | tf_op jit(solution)/shard_map/while
  124.3 13.2 %copy-start.16 = (s32[2,16,144]{2,1,0:T(8,128)S(1)}, s32[2,16,144]{2,1,0:T(8,128)}, u32[]{:S(2)}) copy-start(s32[2,16,144]{2,1,0:T(8,128)} %get-tuple-element.330) | copy-start | bytes 55300 | tf_op jit(solution)/shard_map/while
  124.3 13.1 %copy-start.19 = (pred[2,16,144]{2,1,0:T(8,128)(4,1)S(1)}, pred[2,16,144]{2,1,0:T(8,128)(4,1)}, u32[]{:S(2)}) copy-start(pred[2,16,144]{2,1,0:T(8,128)(4,1)} %get-tuple-element.331) | copy-start | bytes 13828 | tf_op jit(solution)/shard_map/while
  153.8 19.3 %copy-start.7 = (f32[16,6,144]{2,1,0:T(8,128)}, f32[16,6,144]{2,1,0:T(8,128)S(1)}, u32[]{:S(2)}) copy-start(f32[16,6,144]{2,1,0:T(8,128)S(1)} %get-tuple-element.290) | copy-start | bytes 165892 | tf_op jit(solution)/shard_map/while
  153.8 9.6 %copy-start.1 = (f32[16,6,144,144]{2,3,1,0:T(8,128)S(1)}, f32[16,6,144,144]{2,3,1,0:T(8,128)}, u32[]{:S(2)}) copy-start(f32[16,6,144,144]{2,3,1,0:T(8,128)} %get-tuple-element.289) | copy-start | bytes 23887876 | tf_op jit(solution)/shard_map/while
  199.7 6.8 %copy-start.15 = (f32[192,576]{1,0:T(8,128)}, f32[192,576]{1,0:T(8,128)S(1)}, u32[]{:S(2)}) copy-start(f32[192,576]{1,0:T(8,128)S(1)} %fusion.133) | copy-start | bytes 1327108 | tf_op jit(solution)/shard_map/while
  199.7 6.8 %copy-start.4 = (bf16[2,16,144,192]{3,2,1,0:T(8,128)(2,1)S(1)}, bf16[2,16,144,192]{3,2,1,0:T(8,128)(2,1)}, u32[]{:S(2)}) copy-start(bf16[2,16,144,192]{3,2,1,0:T(8,128)(2,1)} %copy-done.3) | copy-start | bytes 5308420 | tf_op jit(solution)/shard_map/while
  199.7 6.8 %copy-start.17 = (f32[192,192]{1,0:T(8,128)S(1)}, f32[192,192]{1,0:T(8,128)}, u32[]{:S(2)}) copy-start(f32[192,192]{1,0:T(8,128)} %get-tuple-element.310) | copy-start | bytes 442372 | tf_op jit(solution)/shard_map/while
  207.2 17.1 %copy-start.18 = (f32[192,192]{1,0:T(8,128)}, f32[192,192]{1,0:T(8,128)S(1)}, u32[]{:S(2)}) copy-start(f32[192,192]{1,0:T(8,128)S(1)} %fusion.135) | copy-start | bytes 442372 | tf_op jit(solution)/shard_map/while
  224.3 34.4 %slice-start = ((s8[4718592]{0:T(1024)(128)(4,1)}), s8[524288]{0:T(1024)(128)(4,1)S(1)}, s32[]{:S(2)}) async-start(s8[4718592]{0:T(1024)(128)(4,1)} %bitcast.188), calls=%async_computation.2 | async-start | bytes 1048576 | tf_op jit(solution)/shard_map/while
  247.5 11.2 %slice-start.1 = ((s8[4718592]{0:T(1024)(128)(4,1)}), s8[4194304]{0:T(1024)(128)(4,1)S(1)}, s32[]{:S(2)}) async-start(s8[4718592]{0:T(1024)(128)(4,1)} %bitcast.188), calls=%async_computation.3 | async-start | bytes 8388608 | tf_op jit(solution)/shard_map/while
  247.5 11.2 %copy-start.6 = (bf16[192,576]{1,0:T(8,128)(2,1)S(1)}, bf16[192,576]{1,0:T(8,128)(2,1)}, u32[]{:S(2)}) copy-start(bf16[192,576]{1,0:T(8,128)(2,1)} %get-tuple-element.329) | copy-start | bytes 663556 | tf_op jit(solution)/shard_map/while
  262.7 18.3 %copy-start.3 = (bf16[2,16,144,192]{3,2,1,0:T(8,128)(2,1)}, bf16[2,16,144,192]{3,2,1,0:T(8,128)(2,1)S(1)}, u32[]{:S(2)}) copy-start(bf16[2,16,144,192]{3,2,1,0:T(8,128)(2,1)S(1)} %get-tuple-element.334) | copy-start | bytes 5308420 | tf_op jit(solution)/shard_map/while
  293.4 17.0 %copy-start.5 = (bf16[192,576]{1,0:T(8,128)(2,1)S(1)}, bf16[192,576]{1,0:T(8,128)(2,1)}, u32[]{:S(2)}) copy-start(bf16[192,576]{1,0:T(8,128)(2,1)} %get-tuple-element.329) | copy-start | bytes 663556 | tf_op jit(solution)/shard_map/while
  317.6 13.1 %copy-start.16 = (s32[2,16,144]{2,1,0:T(8,128)S(1)}, s32[2,16,144]{2,1,0:T(8,128)}, u32[]{:S(2)}) copy-start(s32[2,16,144]{2,1,0:T(8,128)} %get-tuple-element.330) | copy-start | bytes 55300 | tf_op jit(solution)/shard_map/while
  317.6 13.1 %copy-start.19 = (pred[2,16,144]{2,1,0:T(8,128)(4,1)S(1)}, pred[2,16,144]{2,1,0:T(8,128)(4,1)}, u32[]{:S(2)}) copy-start(pred[2,16,144]{2,1,0:T(8,128)(4,1)} %get-tuple-element.331) | copy-start | bytes 13828 | tf_op jit(solution)/shard_map/while
  347.1 19.3 %copy-start.7 = (f32[16,6,144]{2,1,0:T(8,128)}, f32[16,6,144]{2,1,0:T(8,128)S(1)}, u32[]{:S(2)}) copy-start(f32[16,6,144]{2,1,0:T(8,128)S(1)} %get-tuple-element.290) | copy-start | bytes 165892 | tf_op jit(solution)/shard_map/while
  347.1 9.6 %copy-start.1 = (f32[16,6,144,144]{2,3,1,0:T(8,128)S(1)}, f32[16,6,144,144]{2,3,1,0:T(8,128)}, u32[]{:S(2)}) copy-start(f32[16,6,144,144]{2,3,1,0:T(8,128)} %get-tuple-element.289) | copy-start | bytes 23887876 | tf_op jit(solution)/shard_map/while
  393.0 6.8 %copy-start.15 = (f32[192,576]{1,0:T(8,128)}, f32[192,576]{1,0:T(8,128)S(1)}, u32[]{:S(2)}) copy-start(f32[192,576]{1,0:T(8,128)S(1)} %fusion.133) | copy-start | bytes 1327108 | tf_op jit(solution)/shard_map/while
  400.5 17.1 %copy-start.18 = (f32[192,192]{1,0:T(8,128)}, f32[192,192]{1,0:T(8,128)S(1)}, u32[]{:S(2)}) copy-start(f32[192,192]{1,0:T(8,128)S(1)} %fusion.135) | copy-start | bytes 442372 | tf_op jit(solution)/shard_map/while
  417.6 36.5 %slice-start = ((s8[4718592]{0:T(1024)(128)(4,1)}), s8[524288]{0:T(1024)(128)(4,1)S(1)}, s32[]{:S(2)}) async-start(s8[4718592]{0:T(1024)(128)(4,1)} %bitcast.188), calls=%async_computation.2 | async-start | bytes 1048576 | tf_op jit(solution)/shard_map/while
  440.8 13.3 %slice-start.1 = ((s8[4718592]{0:T(1024)(128)(4,1)}), s8[4194304]{0:T(1024)(128)(4,1)S(1)}, s32[]{:S(2)}) async-start(s8[4718592]{0:T(1024)(128)(4,1)} %bitcast.188), calls=%async_computation.3 | async-start | bytes 8388608 | tf_op jit(solution)/shard_map/while
  440.8 13.3 %copy-start.6 = (bf16[192,576]{1,0:T(8,128)(2,1)S(1)}, bf16[192,576]{1,0:T(8,128)(2,1)}, u32[]{:S(2)}) copy-start(bf16[192,576]{1,0:T(8,128)(2,1)} %get-tuple-element.329) | copy-start | bytes 663556 | tf_op jit(solution)/shard_map/while
  469.2 143.3 %all-reduce.5.cloned.1.call-start = ((), (), s32[]{:S(2)}) async-start(), calls=%async_computation | async-start | bytes 11304960 | tf_op jit(solution)/shard_map/psum | solution.py:190
  519.7 8.3 %collective-permute-start.4 = (bf16[8,3,24,192]{3,0,2,1:T(8,128)(2,1)S(1)}, bf16[8,3,24,192]{3,0,2,1:T(8,128)(2,1)S(1)}, u32[]{:S(2)}, u32[]{:S(2)}) collective-permute-start(bf16[8,3,24,192]{3,0,2,1:T(8,128)(2,1)S(1)} %slice.99), channel_id=1, source_target_pairs={{0,1},{1,2},{2,3},{4,5},{5,6},{6,7},{8,9},{9,10},{10,11},{12,13},{... | collective-permute-start | bytes 663560 | tf_op jit(solution)/shard_map/ppermute | solution.py:22
  528.1 19.4 %collective-permute-start.5 = (bf16[8,24,6,192]{3,0,2,1:T(8,128)(2,1)S(1)}, bf16[8,24,6,192]{3,0,2,1:T(8,128)(2,1)S(1)}, u32[]{:S(2)}, u32[]{:S(2)}) collective-permute-start(bf16[8,24,6,192]{3,0,2,1:T(8,128)(2,1)S(1)} %pad_maximum_fusion.7), channel_id=1, source_target_pairs={{28,0},{0,4},{4,8},{8,12},{12,16},{16,20},{20,24},{24,28},{29,1},{... | collective-permute-start | bytes 1327112 | tf_op jit(solution)/shard_map/ppermute | solution.py:16
  (22 other events, 71.5 us)
Sparse Core Ops, SparseCore 0:
  469.3 36.3 all-reduce.6
  510.0 102.4 all-reduce.4
where the time goes:
time: 635 us; the launch traced here: 629 us
  local copies, waits for them, and re-layouts  244 us (38%)
  matrix products  161 us (25%)
  waiting for transfers between devices  110 us (17%)
  other arithmetic  79.9 us (13%)
  between operations  14.5 us (2%)
  starting transfers between devices  11.1 us (2%)
  loops' own time  9.27 us (1%)
    dot_general x4, local copies, waits for them, and re-layouts, window_backward(): jnp.dot(block_types.astype(jnp.bfloat16), bias_rows, preferred_element_ty...  64.3 us
    psum x1, waiting for transfers between devices, local(): lax.psum(totals[2].astype(jnp.bfloat16), 'lon').astype(jnp.float32)  61.7 us
    reshape x2, local copies, waits for them, and re-layouts, window_backward(): score_grad.reshape(windows, -1)  46.5 us
    mul x2, local copies, waits for them, and re-layouts, window_backward(): score_grad = attn_probs * (prob_grad - row_delta)  34.2 us
    sub x2, other arithmetic, window_backward(): exp_terms = jnp.where(allowed, jnp.exp(scores - peak_score), 0.0)  30.7 us
    dot_general x2, matrix products, window_backward(): jnp.einsum('bqhd,bkhd->bhqk', queries, key_rows, preferred_element_type=f32)  26.3 us
    dot_general x2, matrix products, window_backward(): jnp.dot(block_types.astype(jnp.bfloat16), bias_rows, preferred_element_ty...  24.7 us
    dot_general x2, matrix products, window_backward(): jnp.dot(block_types.T, score_grad.reshape(windows, -1), precision=high, p...  24.4 us
  transfers between devices with their start and end apart: 8, of which 5 were waited for; matrix products, arithmetic and copies ran while one was open for 10% of the time, Pallas kernels for 0%

commit v1 on v0

--- a/solution.py
+++ b/solution.py
@@ -187,7 +187,9 @@
         lax.psum(totals[1].astype(jnp.bfloat16), "lat").astype(jnp.float32),
     )
     bias_grad, qkv_grad, proj_grad = (
-        lax.psum(totals[2].astype(jnp.bfloat16), "lon").astype(jnp.float32),
+        lax.all_gather(totals[2].astype(jnp.bfloat16), axis_name="lon")
+        .sum(axis=0)
+        .astype(jnp.float32),
         lax.psum(lat_qkv.astype(jnp.bfloat16), "lon").astype(jnp.float32),
         lax.psum(lat_proj.astype(jnp.bfloat16), "lon").astype(jnp.float32),
     )

time: 635 us -> 750 us (1.18)
  waiting for transfers between devices: 110 us -> 218 us
  other arithmetic: 79.9 us -> 97.3 us
  local copies, waits for them, and re-layouts: 244 us -> 235 us
    all_gather x0 -> x1, waiting for transfers between devices: none -> 150 us  [local(): lax.all_gather(totals[2].astype(jnp.bfloat16), axis_name='lon').sum(axis=0)]
    psum x1, waiting for transfers between devices: 61.7 us -> 26.3 us  [local(): lax.psum(lat_qkv.astype(jnp.bfloat16), 'lon').astype(jnp.float32)]
    ppermute x3, waiting for transfers between devices: 19.4 us -> 0.01 us  [from_behind(): return lax.ppermute(block, axis, route)]
    psum x1, waiting for transfers between devices: 21.9 us -> 36.5 us  [local(): lax.psum(totals[0].astype(jnp.bfloat16), 'lat').astype(jnp.float32)]
    reduce_sum x0 -> x1, other arithmetic: none -> 14 us  [local(): bias_grad, qkv_grad, proj_grad = (lax.all_gather(totals[2].astype(jnp.bfl...]
    reshape x1 -> x0, local copies, waits for them, and re-layouts: 9.01 us -> none  [local(): bias_grad.reshape(types_local, HEADS, WTOK * WTOK)]
    unnamed x16 -> x17, local copies, waits for them, and re-layouts: 24.1 us -> 19 us
  transfers between devices with their start and end apart: 8 -> 9, of which waited for: 5 -> 5; matrix products, arithmetic and copies ran while one was open for 10% -> 8% of each run, Pallas kernels for 0% -> 0%
where the time goes in v1:
time: 750 us; the launch traced here: 745 us
  local copies, waits for them, and re-layouts  235 us (31%)
  waiting for transfers between devices  218 us (29%)
  matrix products  161 us (21%)
  other arithmetic  97.3 us (13%)
  between operations  14.2 us (2%)
  starting transfers between devices  11.1 us (1%)
  loops' own time  8.51 us (1%)
    all_gather x1, waiting for transfers between devices, local(): lax.all_gather(totals[2].astype(jnp.bfloat16), axis_name='lon').sum(axis=0)  150 us
    dot_general x4, local copies, waits for them, and re-layouts, window_backward(): jnp.dot(block_types.astype(jnp.bfloat16), bias_rows, preferred_element_ty...  64.3 us
    reshape x2, local copies, waits for them, and re-layouts, window_backward(): score_grad.reshape(windows, -1)  46.5 us
    psum x1, waiting for transfers between devices, local(): lax.psum(totals[0].astype(jnp.bfloat16), 'lat').astype(jnp.float32)  36.5 us
    mul x2, local copies, waits for them, and re-layouts, window_backward(): score_grad = attn_probs * (prob_grad - row_delta)  34.2 us
    sub x2, other arithmetic, window_backward(): exp_terms = jnp.where(allowed, jnp.exp(scores - peak_score), 0.0)  30.7 us
    psum x1, waiting for transfers between devices, local(): lax.psum(lat_qkv.astype(jnp.bfloat16), 'lon').astype(jnp.float32)  26.3 us
    dot_general x2, matrix products, window_backward(): jnp.einsum('bqhd,bkhd->bhqk', queries, key_rows, preferred_element_type=f32)  26.3 us
  transfers between devices with their start and end apart: 9, of which 5 were waited for; matrix products, arithmetic and copies ran while one was open for 8% of the time, Pallas kernels for 0%

profile of v1, /device:TPU:0, one launch (start us, length us, event | category | flops | bytes accessed | tf_op | source)
XLA Modules:
  0.0 744.8 jit_solution(4067239483443858113)
XLA Ops:
  69.0 396.1 %while.17 = (s32[]{:T(128)}, f32[192,576]{1,0:T(8,128)}, f32[192,192]{1,0:T(8,128)}, f32[16,124416]{1,0:T(8,128)}, bf16[2,16,144,192]{3,1,0,2:T(8,128)(2,1)}, /*...) while((s32[]{:T(128)}, f32[192,576]{1,0:T(8,128)}, ...), condition=%wide.region_4.5_spmd.clone, body=%wide.region_0.4_spmd.clone.sunk | while | flops 3127491072 | bytes 382142976 | solution.py:178
  72.4 15.1 %dot_general.59 = bf16[6,144,144,16]{2,1,0,3:T(8,128)(2,1)} reshape(bf16[124416,16]{0,1:T(8,128)(2,1)} %bitcast.197) | data formatting | bytes 7962624 | tf_op jit(solution)/shard_map/while/body/eval_jaxpr/dot_general | solution.py:60
  87.5 12.4 %fusion.128 = f32[16,6,144,144]{3,0,2,1:T(8,128)} fusion(bf16[6,144,144,16]{2,1,0,3:T(8,128)(2,1)} %dot_general.59, f32[2,16,16]{2,1,0:T(8,128)S(1)} %get-tuple-element.331, s32[]{:T(128)S(6)} %copy.173), kind=kOutput, calls=%fused_computation.8.clone.1 | convolution fusion | flops 63700992 | bytes 11948036 | tf_op jit(solution)/shard_map/while/body/eval_jaxpr/dot_general | solution.py:60
  99.9 17.0 %copy.161 = f32[16,6,144,144]{2,3,1,0:T(8,128)} copy(f32[16,6,144,144]{3,0,2,1:T(8,128)} %fusion.128) | data formatting | bytes 15925248 | tf_op jit(solution)/shard_map/while/body/eval_jaxpr/dot_general | solution.py:60
  119.3 5.1 copy.162
  124.4 13.1 %multiply_add_fusion.2 = f32[16,6,144,144]{2,3,1,0:T(8,128)} fusion(f32[16,6,144,144]{2,3,1,0:T(8,128)} %copy.161, bf16[16,144,3,6,32]{1,4,3,2,0:T(8,128)(2,1)} %bitcast.187), kind=kOutput, calls=%fused_computation.7.clone.1 | convolution fusion | flops 131383296 | bytes 25264128 | tf_op jit(solution)/shard_map/while/body/eval_jaxpr/bqhd,bkhd->bhqk/dot_general | solution.py:64
  138.5 15.3 %fusion.129 = (f32[16,6,144]{2,1,0:T(8,128)S(1)}, f32[16,6,144,144]{2,3,1,0:T(8,128)}) fusion(f32[16,6,144,144]{2,3,1,0:T(8,128)} %multiply_add_fusion.2, pred[16,144,144]{1,2,0:T(8,128)(4,1)S(1)} %compare_and_fusion.2), kind=kOutput, calls=%fused_computation.94.clone.1 | output fusion | flops 7962767 | bytes 16312320 | tf_op jit(solution)/shard_map/while/body/eval_jaxpr/sub | solution.py:72
  153.9 8.0 %fusion.130 = bf16[16,144,1,6,32]{1,4,3,0,2:T(8,128)(2,1)S(1)} fusion(bf16[16,144,6,32]{1,3,2,0:T(8,128)(2,1)} %bitcast.198, f32[16,6,144,144]{2,3,1,0:T(8,128)} %get-tuple-element.288, f32[16,6,144]{2,1,0:T(8,128)S(1)} %get-tuple-element.289), kind=kOutput, calls=%fused_computation.33.clone.1 | convolution fusion | flops 131825664 | bytes 9787392 | tf_op jit(solution)/shard_map/while/body/eval_jaxpr/bhqk,bqhd->bkhd/dot_general | solution.py:99
  163.4 9.7 %multiply_reduce_fusion.2 = (f32[16,6,144]{2,1,0:T(8,128)S(1)}, f32[16,6,144,144]{2,3,1,0:T(8,128)}) fusion(f32[16,6,144,144]{2,3,1,0:T(8,128)S(1)} %copy-done.1, f32[16,6,144]{2,1,0:T(8,128)S(1)} %get-tuple-element.289, bf16[16,144,6,32]{1,3,2,0:T(8,128)(2,1)} %bitcast.199, bf16[16,144,3,6,32]{1,4,3,2,0:T(8,128)(2,1)} %bitcast.188), kind=kOutput, calls=%fused_computation.3.clone.1 | convolution fusion | flops 133360128 | bytes 19181568 | tf_op jit(solution)/shard_map/while/body/eval_jaxpr/bqhd,bkhd->bhqk/dot_general | solution.py:84
  173.1 10.1 %subtract_multiply_fusion.2 = f32[16,6,144,144]{2,3,1,0:T(8,128)S(1)} fusion(f32[16,6,144,144]{2,3,1,0:T(8,128)} %get-tuple-element.290, f32[16,6,144]{2,1,0:T(8,128)S(1)} %get-tuple-element.291, f32[16,6,144,144]{2,3,1,0:T(8,128)} %get-tuple-element.288, f32[16,6,144]{2,1,0:T(8,128)S(1)} %get-tuple-element.289), kind=kLoop, calls=%fused_computation.2.clone.1 | loop fusion | flops 5971968 | bytes 23998464 | tf_op jit(solution)/shard_map/while/body/eval_jaxpr/mul | solution.py:86
  199.8 6.8 fusion.134
  207.2 17.1 %copy.164 = f32[16,6,144,144]{3,2,1,0:T(8,128)} copy(f32[16,6,144,144]{2,3,1,0:T(8,128)} %copy-done) | data formatting | bytes 15925248 | tf_op jit(solution)/shard_map/while/body/eval_jaxpr/mul | solution.py:86
  224.3 23.2 %reshape.130 = f32[16,124416]{1,0:T(8,128)} reshape(f32[16,6,144,144]{3,2,1,0:T(8,128)} %copy.164) | data formatting | bytes 15925248 | tf_op jit(solution)/shard_map/while/body/eval_jaxpr/reshape | solution.py:88
  247.6 11.2 %convolution_add_fusion.2 = f32[16,124416]{1,0:T(8,128)} fusion(f32[16,124416]{1,0:T(8,128)} %reshape.130, f32[16,124416]{1,0:T(8,128)} %get-tuple-element.310, pred[]{:T(512)S(6)} %compare.3, f32[2,16,16]{2,1,0:T(8,128)S(1)} %get-tuple-element.331, s32[]{:T(128)S(6)} %copy.173), kind=kOutput, calls=%fused_computation.1.clone.1 | convolution fusion | flops 386187264 | bytes 23896068 | tf_op jit(solution)/shard_map/while/body/eval_jaxpr/dot_general | solution.py:87
  265.9 15.1 %dot_general.59 = bf16[6,144,144,16]{2,1,0,3:T(8,128)(2,1)} reshape(bf16[124416,16]{0,1:T(8,128)(2,1)} %bitcast.197) | data formatting | bytes 7962624 | tf_op jit(solution)/shard_map/while/body/eval_jaxpr/dot_general | solution.py:60
  281.1 12.4 %fusion.128 = f32[16,6,144,144]{3,0,2,1:T(8,128)} fusion(bf16[6,144,144,16]{2,1,0,3:T(8,128)(2,1)} %dot_general.59, f32[2,16,16]{2,1,0:T(8,128)S(1)} %get-tuple-element.331, s32[]{:T(128)S(6)} %copy.173), kind=kOutput, calls=%fused_computation.8.clone.1 | convolution fusion | flops 63700992 | bytes 11948036 | tf_op jit(solution)/shard_map/while/body/eval_jaxpr/dot_general | solution.py:60
  293.4 17.0 %copy.161 = f32[16,6,144,144]{2,3,1,0:T(8,128)} copy(f32[16,6,144,144]{3,0,2,1:T(8,128)} %fusion.128) | data formatting | bytes 15925248 | tf_op jit(solution)/shard_map/while/body/eval_jaxpr/dot_general | solution.py:60
  317.7 13.1 %multiply_add_fusion.2 = f32[16,6,144,144]{2,3,1,0:T(8,128)} fusion(f32[16,6,144,144]{2,3,1,0:T(8,128)} %copy.161, bf16[16,144,3,6,32]{1,4,3,2,0:T(8,128)(2,1)} %bitcast.187), kind=kOutput, calls=%fused_computation.7.clone.1 | convolution fusion | flops 131383296 | bytes 25264128 | tf_op jit(solution)/shard_map/while/body/eval_jaxpr/bqhd,bkhd->bhqk/dot_general | solution.py:64
  331.8 15.3 %fusion.129 = (f32[16,6,144]{2,1,0:T(8,128)S(1)}, f32[16,6,144,144]{2,3,1,0:T(8,128)}) fusion(f32[16,6,144,144]{2,3,1,0:T(8,128)} %multiply_add_fusion.2, pred[16,144,144]{1,2,0:T(8,128)(4,1)S(1)} %compare_and_fusion.2), kind=kOutput, calls=%fused_computation.94.clone.1 | output fusion | flops 7962767 | bytes 16312320 | tf_op jit(solution)/shard_map/while/body/eval_jaxpr/sub | solution.py:72
  347.2 8.1 %fusion.130 = bf16[16,144,1,6,32]{1,4,3,0,2:T(8,128)(2,1)S(1)} fusion(bf16[16,144,6,32]{1,3,2,0:T(8,128)(2,1)} %bitcast.198, f32[16,6,144,144]{2,3,1,0:T(8,128)} %get-tuple-element.288, f32[16,6,144]{2,1,0:T(8,128)S(1)} %get-tuple-element.289), kind=kOutput, calls=%fused_computation.33.clone.1 | convolution fusion | flops 131825664 | bytes 9787392 | tf_op jit(solution)/shard_map/while/body/eval_jaxpr/bhqk,bqhd->bkhd/dot_general | solution.py:99
  356.7 9.7 %multiply_reduce_fusion.2 = (f32[16,6,144]{2,1,0:T(8,128)S(1)}, f32[16,6,144,144]{2,3,1,0:T(8,128)}) fusion(f32[16,6,144,144]{2,3,1,0:T(8,128)S(1)} %copy-done.1, f32[16,6,144]{2,1,0:T(8,128)S(1)} %get-tuple-element.289, bf16[16,144,6,32]{1,3,2,0:T(8,128)(2,1)} %bitcast.199, bf16[16,144,3,6,32]{1,4,3,2,0:T(8,128)(2,1)} %bitcast.188), kind=kOutput, calls=%fused_computation.3.clone.1 | convolution fusion | flops 133360128 | bytes 19181568 | tf_op jit(solution)/shard_map/while/body/eval_jaxpr/bqhd,bkhd->bhqk/dot_general | solution.py:84
  366.4 10.1 %subtract_multiply_fusion.2 = f32[16,6,144,144]{2,3,1,0:T(8,128)S(1)} fusion(f32[16,6,144,144]{2,3,1,0:T(8,128)} %get-tuple-element.290, f32[16,6,144]{2,1,0:T(8,128)S(1)} %get-tuple-element.291, f32[16,6,144,144]{2,3,1,0:T(8,128)} %get-tuple-element.288, f32[16,6,144]{2,1,0:T(8,128)S(1)} %get-tuple-element.289), kind=kLoop, calls=%fused_computation.2.clone.1 | loop fusion | flops 5971968 | bytes 23998464 | tf_op jit(solution)/shard_map/while/body/eval_jaxpr/mul | solution.py:86
  393.1 6.8 fusion.134
  400.6 17.1 %copy.164 = f32[16,6,144,144]{3,2,1,0:T(8,128)} copy(f32[16,6,144,144]{2,3,1,0:T(8,128)} %copy-done) | data formatting | bytes 15925248 | tf_op jit(solution)/shard_map/while/body/eval_jaxpr/mul | solution.py:86
  417.7 23.2 %reshape.130 = f32[16,124416]{1,0:T(8,128)} reshape(f32[16,6,144,144]{3,2,1,0:T(8,128)} %copy.164) | data formatting | bytes 15925248 | tf_op jit(solution)/shard_map/while/body/eval_jaxpr/reshape | solution.py:88
  440.9 13.3 %convolution_add_fusion.2 = f32[16,124416]{1,0:T(8,128)} fusion(f32[16,124416]{1,0:T(8,128)} %reshape.130, f32[16,124416]{1,0:T(8,128)} %get-tuple-element.310, pred[]{:T(512)S(6)} %compare.3, f32[2,16,16]{2,1,0:T(8,128)S(1)} %get-tuple-element.331, s32[]{:T(128)S(6)} %copy.173), kind=kOutput, calls=%fused_computation.1.clone.1 | convolution fusion | flops 386187264 | bytes 23896068 | tf_op jit(solution)/shard_map/while/body/eval_jaxpr/dot_general | solution.py:87
  468.5 36.5 %all-reduce.7.cloned.1.call-done = (bf16[192,576]{1,0:T(8,128)(2,1)}, bf16[192,192]{1,0:T(8,128)(2,1)}) async-done(((bf16[192,576]{1,0:T(8,128)(2,1)}, bf16[192,192]{1,0:T(8,128)(2,1)}), (bf16[192,576]{1,0:T(8,128)(2,1)}, bf16[192,192]{1,0:T(8,128)(2,1)})) %all-reduce.7.cloned.1.call-update) | async-done | bytes 294928 | tf_op jit(solution)/shard_map/psum | solution.py:186
  505.1 5.6 convert_element_type.90
  519.5 5.0 reshape.114
  535.2 26.3 %all-reduce.5.cloned.1.call-done = (bf16[192,576]{1,0:T(8,128)(2,1)}, bf16[192,192]{1,0:T(8,128)(2,1)}) async-done(((bf16[192,576]{1,0:T(8,128)(2,1)}, bf16[192,192]{1,0:T(8,128)(2,1)}), (bf16[192,576]{1,0:T(8,128)(2,1)}, bf16[192,192]{1,0:T(8,128)(2,1)})) %all-reduce.5.cloned.1.call-update) | async-done | bytes 294928 | tf_op jit(solution)/shard_map/psum | solution.py:193
  568.1 149.5 %all-gather.3.cloned.1.call-done = bf16[128,124416]{1,0:T(8,128)(2,1)} async-done(((bf16[16,124416]{1,0:T(8,128)(2,1)}), bf16[128,124416]{1,0:T(8,128)(2,1)}) %all-gather.3.cloned.1.call-update) | async-done | bytes 31850512 | tf_op jit(solution)/shard_map/all_gather | solution.py:190
  717.6 14.0 %reduce_sum.30 = bf16[16,124416]{1,0:T(8,128)(2,1)} reduce(bf16[8,16,124416]{2,1,0:T(8,128)(2,1)} %bitcast.200, bf16[]{:T(256)} %constant.26.clone.1), dimensions={0}, to_apply=%region_9.10 | reduce | flops 13934592 | bytes 35831808 | tf_op jit(solution)/shard_map/reduce_sum | solution.py:191
  (198 shorter events, 159.7 us)
Async XLA Ops:
  7.2 497.9 %all-reduce.7.cloned.1.call-start = ((), (), s32[]{:S(2)}) async-start(), calls=%async_computation.2 | async-start | bytes 688128 | tf_op jit(solution)/shard_map/psum | solution.py:186
  10.1 20.2 %collective-permute-start = (bf16[8,24,6,192]{3,1,2,0:T(8,128)(2,1)}, bf16[8,24,6,192]{3,1,2,0:T(8,128)(2,1)}, u32[]{:S(2)}, u32[]{:S(2)}) collective-permute-start(bf16[8,24,6,192]{3,1,2,0:T(8,128)(2,1)} %slice.92), channel_id=1, source_target_pairs={{4,0},{8,4},{12,8},{16,12},{20,16},{24,20},{28,24},{0,28},{5,1},{9... | collective-permute-start | bytes 1327112 | tf_op jit(solution)/shard_map/ppermute | solution.py:16
  16.8 15.9 %collective-permute-start.2 = (bf16[8,24,6,192]{3,1,2,0:T(8,128)(2,1)}, bf16[8,24,6,192]{3,1,2,0:T(8,128)(2,1)}, u32[]{:S(2)}, u32[]{:S(2)}) collective-permute-start(bf16[8,24,6,192]{3,1,2,0:T(8,128)(2,1)} %slice.96), channel_id=1, source_target_pairs={{4,0},{8,4},{12,8},{16,12},{20,16},{24,20},{28,24},{0,28},{5,1},{9... | collective-permute-start | bytes 1327112 | tf_op jit(solution)/shard_map/ppermute | solution.py:16
  31.4 11.8 %collective-permute-start.1 = (bf16[8,3,24,192]{3,2,1,0:T(8,128)(2,1)S(1)}, bf16[8,3,24,192]{3,2,1,0:T(8,128)(2,1)S(1)}, u32[]{:S(2)}, u32[]{:S(2)}) collective-permute-start(bf16[8,3,24,192]{3,2,1,0:T(8,128)(2,1)S(1)} %copy.101), channel_id=1, source_target_pairs={{1,0},{2,1},{3,2},{5,4},{6,5},{7,6},{9,8},{10,9},{11,10},{13,12},{... | collective-permute-start | bytes 663560 | tf_op jit(solution)/shard_map/ppermute | solution.py:22
  34.6 18.7 %collective-permute-start.3 = (bf16[8,3,24,192]{3,2,1,0:T(8,128)(2,1)}, bf16[8,3,24,192]{3,2,1,0:T(8,128)(2,1)}, u32[]{:S(2)}, u32[]{:S(2)}) collective-permute-start(bf16[8,3,24,192]{3,2,1,0:T(8,128)(2,1)} %copy.108), channel_id=1, source_target_pairs={{1,0},{2,1},{3,2},{5,4},{6,5},{7,6},{9,8},{10,9},{11,10},{13,12},{... | collective-permute-start | bytes 663560 | tf_op jit(solution)/shard_map/ppermute | solution.py:22
  69.2 18.3 %copy-start.3 = (bf16[2,16,144,192]{3,2,1,0:T(8,128)(2,1)}, bf16[2,16,144,192]{3,2,1,0:T(8,128)(2,1)S(1)}, u32[]{:S(2)}) copy-start(bf16[2,16,144,192]{3,2,1,0:T(8,128)(2,1)S(1)} %get-tuple-element.333) | copy-start | bytes 5308420 | tf_op jit(solution)/shard_map/while
  99.9 17.0 %copy-start.5 = (bf16[192,576]{1,0:T(8,128)(2,1)S(1)}, bf16[192,576]{1,0:T(8,128)(2,1)}, u32[]{:S(2)}) copy-start(bf16[192,576]{1,0:T(8,128)(2,1)} %get-tuple-element.328) | copy-start | bytes 663556 | tf_op jit(solution)/shard_map/while
  124.4 13.1 %copy-start.17 = (s32[2,16,144]{2,1,0:T(8,128)S(1)}, s32[2,16,144]{2,1,0:T(8,128)}, u32[]{:S(2)}) copy-start(s32[2,16,144]{2,1,0:T(8,128)} %get-tuple-element.329) | copy-start | bytes 55300 | tf_op jit(solution)/shard_map/while
  124.4 13.1 %copy-start.20 = (pred[2,16,144]{2,1,0:T(8,128)(4,1)S(1)}, pred[2,16,144]{2,1,0:T(8,128)(4,1)}, u32[]{:S(2)}) copy-start(pred[2,16,144]{2,1,0:T(8,128)(4,1)} %get-tuple-element.330) | copy-start | bytes 13828 | tf_op jit(solution)/shard_map/while
  153.9 19.3 %copy-start.7 = (f32[16,6,144]{2,1,0:T(8,128)}, f32[16,6,144]{2,1,0:T(8,128)S(1)}, u32[]{:S(2)}) copy-start(f32[16,6,144]{2,1,0:T(8,128)S(1)} %get-tuple-element.289) | copy-start | bytes 165892 | tf_op jit(solution)/shard_map/while
  153.9 9.6 %copy-start.1 = (f32[16,6,144,144]{2,3,1,0:T(8,128)S(1)}, f32[16,6,144,144]{2,3,1,0:T(8,128)}, u32[]{:S(2)}) copy-start(f32[16,6,144,144]{2,3,1,0:T(8,128)} %get-tuple-element.288) | copy-start | bytes 23887876 | tf_op jit(solution)/shard_map/while
  199.8 6.8 copy-start.16
  207.2 17.1 %copy-start.19 = (f32[192,192]{1,0:T(8,128)}, f32[192,192]{1,0:T(8,128)S(1)}, u32[]{:S(2)}) copy-start(f32[192,192]{1,0:T(8,128)S(1)} %fusion.135) | copy-start | bytes 442372 | tf_op jit(solution)/shard_map/while
  224.3 34.4 %slice-start = ((s8[4718592]{0:T(1024)(128)(4,1)}), s8[524288]{0:T(1024)(128)(4,1)S(1)}, s32[]{:S(2)}) async-start(s8[4718592]{0:T(1024)(128)(4,1)} %bitcast.193), calls=%async_computation.3 | async-start | bytes 1048576 | tf_op jit(solution)/shard_map/while
  247.6 11.2 %slice-start.1 = ((s8[4718592]{0:T(1024)(128)(4,1)}), s8[4194304]{0:T(1024)(128)(4,1)S(1)}, s32[]{:S(2)}) async-start(s8[4718592]{0:T(1024)(128)(4,1)} %bitcast.193), calls=%async_computation.4 | async-start | bytes 8388608 | tf_op jit(solution)/shard_map/while
  247.6 11.2 %copy-start.6 = (bf16[192,576]{1,0:T(8,128)(2,1)S(1)}, bf16[192,576]{1,0:T(8,128)(2,1)}, u32[]{:S(2)}) copy-start(bf16[192,576]{1,0:T(8,128)(2,1)} %get-tuple-element.328) | copy-start | bytes 663556 | tf_op jit(solution)/shard_map/while
  262.7 18.3 %copy-start.3 = (bf16[2,16,144,192]{3,2,1,0:T(8,128)(2,1)}, bf16[2,16,144,192]{3,2,1,0:T(8,128)(2,1)S(1)}, u32[]{:S(2)}) copy-start(bf16[2,16,144,192]{3,2,1,0:T(8,128)(2,1)S(1)} %get-tuple-element.333) | copy-start | bytes 5308420 | tf_op jit(solution)/shard_map/while
  293.4 17.0 %copy-start.5 = (bf16[192,576]{1,0:T(8,128)(2,1)S(1)}, bf16[192,576]{1,0:T(8,128)(2,1)}, u32[]{:S(2)}) copy-start(bf16[192,576]{1,0:T(8,128)(2,1)} %get-tuple-element.328) | copy-start | bytes 663556 | tf_op jit(solution)/shard_map/while
  317.7 13.1 %copy-start.17 = (s32[2,16,144]{2,1,0:T(8,128)S(1)}, s32[2,16,144]{2,1,0:T(8,128)}, u32[]{:S(2)}) copy-start(s32[2,16,144]{2,1,0:T(8,128)} %get-tuple-element.329) | copy-start | bytes 55300 | tf_op jit(solution)/shard_map/while
  317.7 13.1 %copy-start.20 = (pred[2,16,144]{2,1,0:T(8,128)(4,1)S(1)}, pred[2,16,144]{2,1,0:T(8,128)(4,1)}, u32[]{:S(2)}) copy-start(pred[2,16,144]{2,1,0:T(8,128)(4,1)} %get-tuple-element.330) | copy-start | bytes 13828 | tf_op jit(solution)/shard_map/while
  347.2 19.3 %copy-start.7 = (f32[16,6,144]{2,1,0:T(8,128)}, f32[16,6,144]{2,1,0:T(8,128)S(1)}, u32[]{:S(2)}) copy-start(f32[16,6,144]{2,1,0:T(8,128)S(1)} %get-tuple-element.289) | copy-start | bytes 165892 | tf_op jit(solution)/shard_map/while
  347.2 9.6 %copy-start.1 = (f32[16,6,144,144]{2,3,1,0:T(8,128)S(1)}, f32[16,6,144,144]{2,3,1,0:T(8,128)}, u32[]{:S(2)}) copy-start(f32[16,6,144,144]{2,3,1,0:T(8,128)} %get-tuple-element.288) | copy-start | bytes 23887876 | tf_op jit(solution)/shard_map/while
  393.1 6.8 copy-start.16
  393.1 6.8 copy-start.4
  400.6 17.1 %copy-start.19 = (f32[192,192]{1,0:T(8,128)}, f32[192,192]{1,0:T(8,128)S(1)}, u32[]{:S(2)}) copy-start(f32[192,192]{1,0:T(8,128)S(1)} %fusion.135) | copy-start | bytes 442372 | tf_op jit(solution)/shard_map/while
  417.7 36.5 %slice-start = ((s8[4718592]{0:T(1024)(128)(4,1)}), s8[524288]{0:T(1024)(128)(4,1)S(1)}, s32[]{:S(2)}) async-start(s8[4718592]{0:T(1024)(128)(4,1)} %bitcast.193), calls=%async_computation.3 | async-start | bytes 1048576 | tf_op jit(solution)/shard_map/while
  440.9 13.3 %slice-start.1 = ((s8[4718592]{0:T(1024)(128)(4,1)}), s8[4194304]{0:T(1024)(128)(4,1)S(1)}, s32[]{:S(2)}) async-start(s8[4718592]{0:T(1024)(128)(4,1)} %bitcast.193), calls=%async_computation.4 | async-start | bytes 8388608 | tf_op jit(solution)/shard_map/while
  440.9 13.3 %copy-start.6 = (bf16[192,576]{1,0:T(8,128)(2,1)S(1)}, bf16[192,576]{1,0:T(8,128)(2,1)}, u32[]{:S(2)}) copy-start(bf16[192,576]{1,0:T(8,128)(2,1)} %get-tuple-element.328) | copy-start | bytes 663556 | tf_op jit(solution)/shard_map/while
  468.5 93.0 %all-reduce.5.cloned.1.call-start = ((), (), s32[]{:S(2)}) async-start(), calls=%async_computation.1 | async-start | bytes 688128 | tf_op jit(solution)/shard_map/psum | solution.py:193
  505.1 212.5 %all-gather.3.cloned.1.call-start = ((), (), s32[]{:S(2)}) async-start(), calls=%async_computation | async-start | bytes 35831808 | tf_op jit(solution)/shard_map/all_gather | solution.py:190
  525.9 8.3 %collective-permute-start.4 = (bf16[8,3,24,192]{3,0,2,1:T(8,128)(2,1)S(1)}, bf16[8,3,24,192]{3,0,2,1:T(8,128)(2,1)S(1)}, u32[]{:S(2)}, u32[]{:S(2)}) collective-permute-start(bf16[8,3,24,192]{3,0,2,1:T(8,128)(2,1)S(1)} %slice.99), channel_id=1, source_target_pairs={{0,1},{1,2},{2,3},{4,5},{5,6},{6,7},{8,9},{9,10},{10,11},{12,13},{... | collective-permute-start | bytes 663560 | tf_op jit(solution)/shard_map/ppermute | solution.py:22
  535.2 29.7 %collective-permute-start.5 = (bf16[8,24,6,192]{3,0,2,1:T(8,128)(2,1)}, bf16[8,24,6,192]{3,0,2,1:T(8,128)(2,1)S(1)}, u32[]{:S(2)}, u32[]{:S(2)}) collective-permute-start(bf16[8,24,6,192]{3,0,2,1:T(8,128)(2,1)} %pad_maximum_fusion.7), channel_id=1, source_target_pairs={{28,0},{0,4},{4,8},{8,12},{12,16},{16,20},{20,24},{24,28},{29,1},{... | collective-permute-start | bytes 1327112 | tf_op jit(solution)/shard_map/ppermute | solution.py:16
  (24 other events, 79.8 us)
Sparse Core Ops, SparseCore 0:
  468.6 36.4 all-reduce.6
  508.3 53.1 all-reduce.4
  563.4 154.1 all-gather.2
